TPU v7x, 32 devices: a whole 2x2x4 slice. The times are simulated.
32 devices in a mesh: seq: 4 (over z), head: 4 (over y, core), batch: 2 (over x).
Axes of the slice: x: 2, y: 2, z: 4, core: 2. Of those that a mesh axis runs over, the one named last changes fastest.
Arguments:
- tokens: bfloat16 [8192, 2048], P(('batch', 'seq')), parts along dimension 0, may hold values from -6 to 6
- neighbor_bank: bfloat16 [128, 256, 2048], P(('batch', 'seq')), parts along dimension 0, may hold values from -2100 to 2100
- slots: int32 [128], P(('batch', 'seq')), parts along dimension 0, may hold values from 0 to 15
- w_query: bfloat16 [2048, 2048], P('seq', 'head'), may hold values from -0.125 to 0.125
- w_key: bfloat16 [2048, 2048], P('seq', 'head'), may hold values from -0.125 to 0.125
- w_value: bfloat16 [2048, 2048], P('seq', 'head'), may hold values from -0.125 to 0.125
- w_out: bfloat16 [2048, 2048], P('head', 'seq'), may hold values from -0.125 to 0.125
Outputs:
- cross_out: bfloat16 [8192, 2048], P(('batch', 'seq'), 'head'), parts along dimension 0
There are 2 independent parts, one for each index of `batch`. A program takes and returns all parts, laid end to end along the dimension named above; an argument that names none is the same for every part. Nothing has to cross between parts.
Inputs may be any that keep to these rules, and one draw needn't show every extreme that they name: Entry c picks row c // 16 * 16 + slots[c] of neighbor_bank.
All inputs are finite; a program needn't handle non-finite values.
Results may differ from a plain program's by a relative error of at most 0.006.
The roundings to bfloat16 on the way count: a program that leaves them out, or rounds other values in their place, can miss the bound.
Values may be sent and summed in bfloat16 or wider, within the bound.
A program may use at most 128 MiB of HBM per device.

v0:
```python
import math
import jax
import jax.numpy as jnp
from jax import lax
from jax.sharding import PartitionSpec as P

HEAD_DIM = 128


def passed_along(block, axis, distance):
    devices = range(lax.axis_size(axis))
    route = [(i - distance, i) for i in devices if i - distance in devices]
    return lax.ppermute(block, axis, route)


def attend(query_blocks, key_blocks, value_blocks):
    scores = jnp.einsum(
        "cmhd,cnhd->chmn", query_blocks, key_blocks, preferred_element_type=jnp.float32
    ) / math.sqrt(HEAD_DIM)
    peak_score = jnp.max(scores, axis=-1, keepdims=True)
    exponent = jnp.exp(scores - peak_score)
    weights = (exponent / jnp.sum(exponent, axis=-1, keepdims=True)).astype(jnp.bfloat16)
    blended = jnp.einsum(
        "chmn,cnhd->cmhd", weights, value_blocks, preferred_element_type=jnp.float32
    ).astype(jnp.bfloat16)
    return blended.reshape(blended.shape[0] * blended.shape[1], blended.shape[2] * blended.shape[3])


def fold_rows(source, shard_rows):
    return jnp.dot(source, shard_rows, preferred_element_type=jnp.float32)


def local(tokens, neighbor_bank, slots, w_query, w_key, w_value, w_out):
    tok_rows, model_width = tokens.shape
    block_count = neighbor_bank.shape[0]
    neighbor_rows = neighbor_bank.shape[1]
    block_len = tok_rows // block_count
    local_width = w_query.shape[1]
    local_heads = local_width // HEAD_DIM
    hidden = tokens.astype(jnp.float32)
    normed = (hidden * lax.rsqrt(jnp.mean(hidden * hidden, axis=-1, keepdims=True) + 1e-06)).astype(
        jnp.bfloat16
    )
    retrieved = jnp.take(neighbor_bank, slots, axis=0)
    arrived = passed_along(retrieved[block_count - 1], "seq", 1)
    context = jnp.concatenate([arrived[None], retrieved[: block_count - 1]], axis=0)
    context_flat = context.reshape(block_count * neighbor_rows, model_width)
    query_sum = fold_rows(normed, lax.all_gather(w_query, "seq", axis=0, tiled=True))
    key_sum = fold_rows(context_flat, lax.all_gather(w_key, "seq", axis=0, tiled=True))
    value_sum = fold_rows(context_flat, lax.all_gather(w_value, "seq", axis=0, tiled=True))
    query_blocks = query_sum.astype(jnp.bfloat16).reshape(
        block_count, block_len, local_heads, HEAD_DIM
    )
    key_blocks = key_sum.astype(jnp.bfloat16).reshape(
        block_count, neighbor_rows, local_heads, HEAD_DIM
    )
    value_blocks = value_sum.astype(jnp.bfloat16).reshape(
        block_count, neighbor_rows, local_heads, HEAD_DIM
    )
    attended = attend(query_blocks, key_blocks, value_blocks)
    every_head = lax.all_gather(attended, "head", axis=1, tiled=True)
    wide_rows = lax.all_gather(w_out, "seq", axis=1, tiled=True)
    own_columns = lax.all_to_all(wide_rows, "head", split_axis=1, concat_axis=0, tiled=True)
    return jnp.dot(every_head, own_columns, preferred_element_type=jnp.float32).astype(jnp.bfloat16)


def solution(mesh):
    in_specs = (
        P(("batch", "seq"), None),
        P(("batch", "seq"), None, None),
        P(("batch", "seq")),
        P("seq", "head"),
        P("seq", "head"),
        P("seq", "head"),
        P("head", "seq"),
    )
    out_specs = P(("batch", "seq"), "head")
    return jax.shard_map(local, mesh=mesh, in_specs=in_specs, out_specs=out_specs, check_vma=False)
```

profile of v0, /device:TPU:0, one launch (start us, length us, event | category | flops | bytes accessed | tf_op | source)
XLA Modules:
  0.0 271.8 jit_solution(8878170851766473111)
XLA Ops:
  6.5 0.0 all-gather.10.cloned.1.call-start
  6.5 0.7 all-gather.10.cloned.1.call-update
  7.3 0.0 all-gather.8.cloned.1.call-start
  7.3 0.7 all-gather.8.cloned.1.call-update
  8.0 0.0 all-gather.6.cloned.1.call-start
  8.1 0.7 all-gather.6.cloned.1.call-update
  8.7 0.0 all-gather.14.cloned.1.call-start
  8.8 0.7 compare_select_fusion
  9.4 0.7 compare_and_fusion
  10.1 13.1 %gather_fusion = bf16[16,256,2048]{2,1,0:T(8,128)(2,1)} fusion(bf16[16,256,2048]{2,1,0:T(8,128)(2,1)} %param.8, s32[1024]{0:T(1024)S(1)} %pad_clamp_fusion), kind=kCustom, calls=%fused_computation | custom fusion | bytes 33554496 | tf_op jit(solution)/shard_map/jit(_take)/gather | solution.py:44
  23.2 0.0 copy-start.3
  23.2 8.6 %broadcast_select_fusion = bf16[16,256,2048]{2,1,0:T(8,128)(2,1)S(1)} fusion(bf16[16,256,2048]{2,1,0:T(8,128)(2,1)} %gather_fusion, pred[16]{0:T(512)(128)(4,1)S(1)} %compare_and_fusion), kind=kLoop, calls=%fused_computation.3 | loop fusion | flops 8388608 | bytes 33554448 | tf_op jit(solution)/shard_map/jit(_take)/select_n | solution.py:44
  31.8 0.0 copy-start
  31.8 5.7 %copy-done = bf16[16,256,2048]{2,1,0:T(8,128)(2,1)} copy-done((bf16[16,256,2048]{2,1,0:T(8,128)(2,1)}, bf16[16,256,2048]{2,1,0:T(8,128)(2,1)S(1)}, u32[]{:S(2)}) %copy-start) | copy-done | bytes 16777240
  37.5 0.1 slice_bitcast_fusion
  37.6 5.0 %collective-permute-start = (bf16[256,2048]{1,0:T(8,128)(2,1)S(1)}, bf16[256,2048]{1,0:T(8,128)(2,1)S(1)}, u32[]{:S(2)}, u32[]{:S(2)}) collective-permute-start(bf16[256,2048]{1,0:T(8,128)(2,1)S(1)} %slice_bitcast_fusion), channel_id=1, source_target_pairs={{0,8},{8,16},{16,24},{1,9},{9,17},{17,25},{2,10},{10,18},{18,26},{... | collective-permute-start | bytes 3145736 | tf_op jit(solution)/shard_map/ppermute | solution.py:13
  42.6 0.0 copy-done.3
  42.6 1.0 copy.19
  43.6 0.0 all-gather.14.cloned.1.call-update
  43.6 0.0 all-gather.12.cloned.1.call-start
  43.7 0.0 copy-start.1
  43.7 0.0 slice-start
  43.7 2.2 copy-done.1
  45.9 0.9 fusion.1
  46.8 31.2 %collective-permute-done = bf16[256,2048]{1,0:T(8,128)(2,1)S(1)} collective-permute-done((bf16[256,2048]{1,0:T(8,128)(2,1)S(1)}, bf16[256,2048]{1,0:T(8,128)(2,1)S(1)}, u32[]{:S(2)}, u32[]{:S(2)}) %collective-permute-start) | collective-permute-done | bytes 1048608 | tf_op jit(solution)/shard_map/ppermute | solution.py:13
  78.0 0.0 slice-done
  78.0 6.6 %pad_maximum_fusion = bf16[16,256,2048]{2,1,0:T(8,128)(2,1)} fusion(bf16[15,256,2048]{2,1,0:T(8,128)(2,1)S(1)} %slice-done, bf16[1,256,2048]{2,1,0:T(8,128)(2,1)S(1)} %bitcast.28), kind=kLoop, calls=%fused_computation.2 | loop fusion | flops 8388608 | bytes 33554432 | tf_op jit(solution)/shard_map/concatenate | solution.py:46
  84.6 0.0 all-gather.10.cloned.1.call-done
  84.6 14.4 %convolution_convert_fusion = bf16[4096,512]{1,0:T(8,128)(2,1)} fusion(bf16[4096,2048]{1,0:T(8,128)(2,1)} %bitcast.21, bf16[2048,512]{1,0:T(8,128)(2,1)} %all-gather.10.cloned.1.call-done), kind=kOutput, calls=%fused_computation.8 | convolution fusion | flops 8592031744 | bytes 23068672 | tf_op jit(solution)/shard_map/dot_general | solution.py:30
  99.0 13.5 %all-gather.8.cloned.1.call-done = bf16[2048,512]{1,0:T(8,128)(2,1)} async-done(((bf16[512,512]{1,0:T(8,128)(2,1)}), bf16[2048,512]{1,0:T(8,128)(2,1)}) %all-gather.8.cloned.1.call-update) | async-done | bytes 2097168 | tf_op jit(solution)/shard_map/all_gather | solution.py:48
  112.5 5.2 %fusion.18 = bf16[1024,512]{1,0:T(8,128)(2,1)S(1)} fusion(bf16[2048,512]{1,0:T(8,128)(2,1)} %all-gather.8.cloned.1.call-done, bf16[1024,2048]{1,0:T(8,128)(2,1)} %param.7, f32[1024]{0:T(1024)S(1)} %add_rsqrt_fusion), kind=kOutput, calls=%fused_computation.23 | convolution fusion | flops 2154299392 | bytes 7344128 | tf_op jit(solution)/shard_map/dot_general | solution.py:30
  117.8 7.0 %reshape.36 = bf16[16,256,4,128]{3,2,1,0:T(4,128)(2,1)} reshape(bf16[4096,512]{1,0:T(8,128)(2,1)} %convolution_convert_fusion) | data formatting | bytes 8388608 | tf_op jit(solution)/shard_map/reshape | solution.py:54
  124.8 0.3 reshape.35
  125.1 34.8 %all-gather.6.cloned.1.call-done = bf16[2048,512]{1,0:T(8,128)(2,1)} async-done(((bf16[512,512]{1,0:T(8,128)(2,1)}), bf16[2048,512]{1,0:T(8,128)(2,1)}) %all-gather.6.cloned.1.call-update) | async-done | bytes 2097168 | tf_op jit(solution)/shard_map/all_gather | solution.py:50
  159.9 14.4 %convolution_convert_fusion.1 = bf16[4096,512]{1,0:T(8,128)(2,1)} fusion(bf16[4096,2048]{1,0:T(8,128)(2,1)} %bitcast.22, bf16[2048,512]{1,0:T(8,128)(2,1)} %all-gather.6.cloned.1.call-done), kind=kOutput, calls=%fused_computation.9 | convolution fusion | flops 8592031744 | bytes 23068672 | tf_op jit(solution)/shard_map/dot_general | solution.py:30
  174.3 7.0 %reshape.34 = bf16[16,256,4,128]{3,2,1,0:T(4,128)(2,1)} reshape(bf16[4096,512]{1,0:T(8,128)(2,1)} %convolution_convert_fusion.1) | data formatting | bytes 8388608 | tf_op jit(solution)/shard_map/reshape | solution.py:57
  181.2 3.8 %fusion.7 = f32[16,4,64,256]{3,2,1,0:T(8,128)S(1)} fusion(bf16[16,256,4,128]{3,2,1,0:T(4,128)(2,1)} %reshape.36, bf16[16,64,4,128]{3,2,1,0:T(4,128)(2,1)S(1)} %reshape.35), kind=kOutput, calls=%fused_computation.13 | convolution fusion | flops 268435456 | bytes 9437184 | tf_op jit(solution)/shard_map/cmhd,cnhd->chmn/dot_general | solution.py:17
  185.0 0.0 copy-start.2
  185.0 2.0 copy-done.2
  187.0 1.6 fusion.33
  188.6 12.0 %fusion.21 = bf16[16,64,4,128]{3,1,2,0:T(8,128)(2,1)S(1)} fusion(bf16[16,256,4,128]{3,2,1,0:T(4,128)(2,1)} %reshape.34, f32[16,4,64]{2,1,0:T(4,128)S(1)} %fusion.33, f32[16,4,64,256]{3,2,1,0:T(8,128)} %copy-done.2), kind=kOutput, calls=%fused_computation.25 | convolution fusion | flops 274206976 | bytes 9453568 | tf_op jit(solution)/shard_map/chmn,cnhd->cmhd/dot_general | solution.py:23
  200.6 0.9 copy.18
  201.5 1.2 copy.33
  202.6 0.0 all-gather.12.cloned.1.call-update
  202.7 3.1 %all-gather.14.cloned.1.call-done = bf16[512,2048]{0,1:T(8,128)(2,1)} async-done(((bf16[512,512]{0,1:T(8,128)(2,1)}), bf16[512,2048]{0,1:T(8,128)(2,1)}) %all-gather.14.cloned.1.call-update) | async-done | bytes 2097168 | tf_op jit(solution)/shard_map/all_gather | solution.py:62
  205.8 48.4 %all_to_all.19 = bf16[512,4,512]{0,2,1:T(8,128)(2,1)S(1)} all-to-all(bf16[512,4,512]{0,2,1:T(8,128)(2,1)} %bitcast.26), channel_id=1, replica_groups=mesh['seq'=4,'head'=4,'batch'=2] {'head'}, dimensions={1} | all-to-all | bytes 4194304 | tf_op jit(solution)/shard_map/all_to_all | solution.py:63
  254.2 2.4 copy.20
  256.6 2.6 all-gather.12.cloned.1.call-done
  259.1 6.2 %convolution_convert_fusion.2 = bf16[1024,512]{1,0:T(8,128)(2,1)} fusion(bf16[1024,2048]{1,0:T(8,128)(2,1)} %all-gather.12.cloned.1.call-done, bf16[2048,512]{1,0:T(8,128)(2,1)} %bitcast.27), kind=kOutput, calls=%fused_computation.24 | convolution fusion | flops 2148007936 | bytes 7340032 | tf_op jit(solution)/shard_map/dot_general | solution.py:64
  (2 shorter events, 0.0 us)
Async XLA Ops:
  6.5 78.0 %all-gather.10.cloned.1.call-start = ((), (), s32[]{:S(2)}) async-start(), calls=%async_computation.3 | async-start | bytes 2621440 | tf_op jit(solution)/shard_map/all_gather | solution.py:49
  7.3 105.3 %all-gather.8.cloned.1.call-start = ((), (), s32[]{:S(2)}) async-start(), calls=%async_computation.2 | async-start | bytes 2621440 | tf_op jit(solution)/shard_map/all_gather | solution.py:48
  8.0 151.9 %all-gather.6.cloned.1.call-start = ((), (), s32[]{:S(2)}) async-start(), calls=%async_computation.1 | async-start | bytes 2621440 | tf_op jit(solution)/shard_map/all_gather | solution.py:50
  8.7 197.1 %all-gather.14.cloned.1.call-start = ((), (), s32[]{:S(2)}) async-start(), calls=%async_computation.5 | async-start | bytes 2621440 | tf_op jit(solution)/shard_map/all_gather | solution.py:62
  23.2 19.4 %copy-start.3 = (bf16[512,512]{1,0:T(8,128)(2,1)S(1)}, bf16[512,512]{1,0:T(8,128)(2,1)}, u32[]{:S(2)}) copy-start(bf16[512,512]{1,0:T(8,128)(2,1)} %param.13) | copy-start | bytes 1572868
  31.8 5.7 %copy-start = (bf16[16,256,2048]{2,1,0:T(8,128)(2,1)}, bf16[16,256,2048]{2,1,0:T(8,128)(2,1)S(1)}, u32[]{:S(2)}) copy-start(bf16[16,256,2048]{2,1,0:T(8,128)(2,1)S(1)} %broadcast_select_fusion) | copy-start | bytes 50331652
  37.6 40.4 %collective-permute-start = (bf16[256,2048]{1,0:T(8,128)(2,1)S(1)}, bf16[256,2048]{1,0:T(8,128)(2,1)S(1)}, u32[]{:S(2)}, u32[]{:S(2)}) collective-permute-start(bf16[256,2048]{1,0:T(8,128)(2,1)S(1)} %slice_bitcast_fusion), channel_id=1, source_target_pairs={{0,8},{8,16},{16,24},{1,9},{9,17},{17,25},{2,10},{10,18},{18,26},{... | collective-permute-start | bytes 3145736 | tf_op jit(solution)/shard_map/ppermute | solution.py:13
  43.6 215.5 %all-gather.12.cloned.1.call-start = ((), (), s32[]{:S(2)}) async-start(), calls=%async_computation.4 | async-start | bytes 5242880 | tf_op jit(solution)/shard_map/all_gather | solution.py:61
  43.7 2.2 copy-start.1
  43.7 34.3 %slice-start = ((bf16[16,256,2048]{2,1,0:T(8,128)(2,1)}), bf16[15,256,2048]{2,1,0:T(8,128)(2,1)S(1)}, s32[]{:S(2)}) async-start(bf16[16,256,2048]{2,1,0:T(8,128)(2,1)} %copy-done), calls=%async_computation.6 | async-start | bytes 31457280 | tf_op jit(solution)/shard_map/slice | solution.py:46
  185.0 2.0 copy-start.2
Sparse Core Ops, SparseCore 0:
  8.9 56.2 all-gather.9
  66.7 45.7 all-gather.7
  114.1 45.7 all-gather.5
  161.3 44.4 all-gather.13
  207.2 51.8 all-gather.11
where the time goes:
time: 272 us
  waiting for transfers between devices  87.4 us (32%)
  matrix products  56 us (21%)
  blocking collectives  48.4 us (18%)
  local copies, waits for them, and re-layouts  42.7 us (16%)
  other arithmetic  19 us (7%)
  between operations  13.2 us (5%)
  starting transfers between devices  5.13 us (2%)
    all_to_all x1, blocking collectives, local(): lax.all_to_all(wide_rows, 'head', split_axis=1, concat_axis=0, tiled=True)  48.4 us
    all_gather x1, waiting for transfers between devices, local(): lax.all_gather(w_value, 'seq', axis=0, tiled=True)  34.8 us
    dot_general x3, matrix products, fold_rows(): return jnp.dot(source, shard_rows, preferred_element_type=jnp.float32)  34 us
    ppermute x1, waiting for transfers between devices, passed_along(): return lax.ppermute(block, axis, route)  31.2 us
    all_gather x1, waiting for transfers between devices, local(): lax.all_gather(w_query, 'seq', axis=0, tiled=True)  13.5 us
    gather x1, local copies, waits for them, and re-layouts, local(): retrieved = jnp.take(neighbor_bank, slots, axis=0)  13.1 us
    unnamed x10, local copies, waits for them, and re-layouts  12.1 us
    dot_general x1, matrix products, attend(): jnp.einsum('chmn,cnhd->cmhd', weights, value_blocks, preferred_element_ty...  12 us
  transfers between devices with their start and end apart: 6, of which 5 were waited for; matrix products, arithmetic and copies ran while one was open for 37% of the time, Pallas kernels for 0%

commit v1 on v0

--- a/solution.py
+++ b/solution.py
@@ -47,7 +47,25 @@
     context_flat = context.reshape(block_count * neighbor_rows, model_width)
     query_sum = fold_rows(normed, lax.all_gather(w_query, "seq", axis=0, tiled=True))
     key_sum = fold_rows(context_flat, lax.all_gather(w_key, "seq", axis=0, tiled=True))
-    value_sum = fold_rows(context_flat, lax.all_gather(w_value, "seq", axis=0, tiled=True))
+
+    def keep_up_flows(x0):
+        how_many = lax.axis_size("seq")
+        near = range(how_many)
+        block_now = map(lambda to_i: (to_i, (to_i + 1) % how_many), near)
+        windows = list(map(lambda to_i: (to_i, (to_i - 1) % how_many), range(how_many)))
+        rows = list(block_now)
+        w_next, low = ([x0], [x0])
+        for _ in range(how_many // 2):
+            built = lax.ppermute(w_next[-1], "seq", rows)
+            w_next.append(built)
+        for _ in range((how_many - 1) // 2):
+            far_arr = lax.ppermute(low[-1], axis_name="seq", perm=windows)
+            low.append(far_arr)
+        outer = jnp.concatenate([*w_next[::-1], *low[1:]], 0)
+        f_now = jnp.roll(outer, (lax.axis_index("seq") - how_many // 2) * x0.shape[0], 0)
+        return f_now
+
+    value_sum = fold_rows(context_flat, keep_up_flows(w_value))
     query_blocks = query_sum.astype(jnp.bfloat16).reshape(
         block_count, block_len, local_heads, HEAD_DIM
     )

time: 272 us -> 253 us (0.930)
  waiting for transfers between devices: 87.4 us -> 48.9 us
  local copies, waits for them, and re-layouts: 42.7 us -> 61.2 us
  matrix products: 56 us -> 52 us
  blocking collectives: 48.4 us -> 44.6 us
  starting transfers between devices: 5.13 us -> 8.33 us
  other arithmetic: 19 us -> 22 us
    ppermute x0 -> x3, waiting for transfers between devices: none -> 41.6 us  [the longest x2 41.6 us: keep_up_flows(): built = lax.ppermute(w_next[-1], 'seq', rows)]
    all_gather x1 -> x0, waiting for transfers between devices: 34.8 us -> none  [local(): lax.all_gather(w_value, 'seq', axis=0, tiled=True)]
    ppermute x1, waiting for transfers between devices: 31.2 us -> 0.01 us  [passed_along(): return lax.ppermute(block, axis, route)]
    all_gather x1, waiting for transfers between devices: 13.5 us -> 0.01 us  [local(): lax.all_gather(w_query, 'seq', axis=0, tiled=True)]
    slice x2 -> x1, local copies, waits for them, and re-layouts: 0.01 us -> 13.5 us  [local(): retrieved[:block_count - 1]]
    ppermute x0 -> x3, starting transfers between devices: none -> 6.61 us  [the longest x2 4.51 us: keep_up_flows(): built = lax.ppermute(w_next[-1], 'seq', rows)]
    dot_general x3, matrix products: 34 us -> 30 us  [fold_rows(): return jnp.dot(source, shard_rows, preferred_element_type=jnp.float32)]
    all_to_all x1, blocking collectives: 48.4 us -> 44.6 us  [local(): lax.all_to_all(wide_rows, 'head', split_axis=1, concat_axis=0, tiled=True)]
  transfers between devices with their start and end apart: 6 -> 8, of which waited for: 5 -> 3; matrix products, arithmetic and copies ran while one was open for 37% -> 46% of each run, Pallas kernels for 0% -> 0%
where the time goes in v1:
time: 253 us; the launch traced here: 250 us
  local copies, waits for them, and re-layouts  61.2 us (24%)
  matrix products  52 us (21%)
  waiting for transfers between devices  48.9 us (19%)
  blocking collectives  44.6 us (18%)
  other arithmetic  22 us (9%)
  between operations  13.3 us (5%)
  starting transfers between devices  8.33 us (3%)
    all_to_all x1, blocking collectives, local(): lax.all_to_all(wide_rows, 'head', split_axis=1, concat_axis=0, tiled=True)  44.6 us
    ppermute x2, waiting for transfers between devices, keep_up_flows(): built = lax.ppermute(w_next[-1], 'seq', rows)  41.6 us
    dot_general x3, matrix products, fold_rows(): return jnp.dot(source, shard_rows, preferred_element_type=jnp.float32)  30 us
    unnamed x21, local copies, waits for them, and re-layouts  15.8 us
    slice x1, local copies, waits for them, and re-layouts, local(): retrieved[:block_count - 1]  13.5 us
    gather x1, local copies, waits for them, and re-layouts, local(): retrieved = jnp.take(neighbor_bank, slots, axis=0)  13.2 us
    dot_general x1, matrix products, attend(): jnp.einsum('chmn,cnhd->cmhd', weights, value_blocks, preferred_element_ty...  12 us
    select_n x2, other arithmetic, local(): retrieved = jnp.take(neighbor_bank, slots, axis=0)  9.29 us
  transfers between devices with their start and end apart: 8, of which 3 were waited for; matrix products, arithmetic and copies ran while one was open for 46% of the time, Pallas kernels for 0%

profile of v1, /device:TPU:0, one launch (start us, length us, event | category | flops | bytes accessed | tf_op | source)
XLA Modules:
  0.0 250.2 jit_solution(359847987553498771)
XLA Ops:
  6.5 0.0 all-gather.7.cloned.1.call-start
  6.5 0.7 all-gather.7.cloned.1.call-update
  7.3 0.0 all-gather.5.cloned.1.call-start
  7.3 3.1 %collective-permute-start.1 = (bf16[512,512]{1,0:T(8,128)(2,1)}, bf16[512,512]{1,0:T(8,128)(2,1)S(1)}, u32[]{:S(2)}, u32[]{:S(2)}) collective-permute-start(bf16[512,512]{1,0:T(8,128)(2,1)} %param.12), channel_id=1, source_target_pairs={{0,8},{8,16},{16,24},{24,0},{1,9},{9,17},{17,25},{25,1},{2,10},{10... | collective-permute-start | bytes 1572872 | tf_op jit(solution)/shard_map/ppermute | solution.py:59
  10.4 2.1 collective-permute-start.3
  12.5 0.0 all-gather.5.cloned.1.call-update
  12.5 0.0 all-gather.11.cloned.1.call-start
  12.6 0.7 compare_select_fusion
  13.2 0.0 copy-start.5
  13.2 13.2 %gather_fusion = bf16[16,256,2048]{2,1,0:T(8,128)(2,1)} fusion(bf16[16,256,2048]{2,1,0:T(8,128)(2,1)} %param.8, s32[1024]{0:T(1024)S(1)} %pad_clamp_fusion), kind=kCustom, calls=%fused_computation | custom fusion | bytes 33554496 | tf_op jit(solution)/shard_map/jit(_take)/gather | solution.py:44
  26.5 0.0 copy-done.5
  26.5 0.0 copy-start.4
  26.5 8.6 %broadcast_select_fusion = bf16[16,256,2048]{2,1,0:T(8,128)(2,1)S(1)} fusion(bf16[16,256,2048]{2,1,0:T(8,128)(2,1)} %gather_fusion, pred[16]{0:T(512)(128)(4,1)S(1)} %compare_and_fusion), kind=kLoop, calls=%fused_computation.3 | loop fusion | flops 8388608 | bytes 33554448 | tf_op jit(solution)/shard_map/jit(_take)/select_n | solution.py:44
  35.2 0.0 copy-start
  35.2 5.7 %copy-done = bf16[16,256,2048]{2,1,0:T(8,128)(2,1)} copy-done((bf16[16,256,2048]{2,1,0:T(8,128)(2,1)}, bf16[16,256,2048]{2,1,0:T(8,128)(2,1)S(1)}, u32[]{:S(2)}) %copy-start) | copy-done | bytes 16777240
  40.9 1.0 slice_bitcast_fusion
  41.9 1.6 collective-permute-start
  43.5 0.0 copy-done.4
  43.6 1.0 copy.19
  44.6 0.0 all-gather.11.cloned.1.call-update
  44.6 0.0 all-gather.9.cloned.1.call-start
  44.6 13.5 %slice.11 = bf16[15,256,2048]{2,1,0:T(8,128)(2,1)} slice(bf16[16,256,2048]{2,1,0:T(8,128)(2,1)} %copy-done), slice={[0:15], [0:256], [0:2048]} | slice | bytes 31457280 | tf_op jit(solution)/shard_map/slice | solution.py:46
  58.1 0.0 copy-start.3
  58.1 0.0 collective-permute-done.1
  58.1 1.4 collective-permute-start.2
  59.5 3.1 %fusion.1 = f32[1024]{0:T(1024)S(1)} fusion(bf16[1024,2048]{1,0:T(8,128)(2,1)} %param.7), kind=kLoop, calls=%fused_computation.6 | loop fusion | flops 6290432 | bytes 4198400 | tf_op jit(solution)/shard_map/reduce_sum | solution.py:41
  62.6 41.6 %collective-permute-done.2 = bf16[512,512]{1,0:T(8,128)(2,1)S(1)} collective-permute-done((bf16[512,512]{1,0:T(8,128)(2,1)S(1)}, bf16[512,512]{1,0:T(8,128)(2,1)S(1)}, u32[]{:S(2)}, u32[]{:S(2)}) %collective-permute-start.2) | collective-permute-done | bytes 524320 | tf_op jit(solution)/shard_map/ppermute | solution.py:59
  104.3 0.0 copy-done.3
  104.3 0.0 collective-permute-done.3
  104.5 0.0 collective-permute-done
  104.5 8.0 %pad_maximum_fusion = bf16[16,256,2048]{2,1,0:T(8,128)(2,1)S(1)} fusion(bf16[15,256,2048]{2,1,0:T(8,128)(2,1)} %slice.11, bf16[1,256,2048]{2,1,0:T(8,128)(2,1)S(1)} %bitcast.27), kind=kLoop, calls=%fused_computation.2 | loop fusion | flops 8388608 | bytes 33554432 | tf_op jit(solution)/shard_map/concatenate | solution.py:46
  112.5 0.0 copy-start.1
  112.6 5.7 %copy-done.1 = bf16[16,256,2048]{2,1,0:T(8,128)(2,1)} copy-done((bf16[16,256,2048]{2,1,0:T(8,128)(2,1)}, bf16[16,256,2048]{2,1,0:T(8,128)(2,1)S(1)}, u32[]{:S(2)}) %copy-start.1) | copy-done | bytes 16777240
  118.3 10.4 %convolution_convert_fusion.1 = bf16[4096,512]{1,0:T(8,128)(2,1)} fusion(bf16[4096,2048]{1,0:T(8,128)(2,1)S(1)} %bitcast.20, bf16[4096,512]{1,0:T(8,128)(2,1)S(1)} %constant_dynamic-update-slice_fusion, s32[]{:T(128)S(6)} %select_n.25), kind=kOutput, calls=%fused_computation.9 | convolution fusion | flops 8592031744 | bytes 23068676 | tf_op jit(solution)/shard_map/dot_general | solution.py:30
  128.7 6.9 %reshape.34 = bf16[16,256,4,128]{3,2,1,0:T(4,128)(2,1)} reshape(bf16[4096,512]{1,0:T(8,128)(2,1)} %convolution_convert_fusion.1) | data formatting | bytes 8388608 | tf_op jit(solution)/shard_map/reshape | solution.py:75
  135.6 0.0 all-gather.7.cloned.1.call-done
  135.6 14.4 %convolution_convert_fusion = bf16[4096,512]{1,0:T(8,128)(2,1)} fusion(bf16[4096,2048]{1,0:T(8,128)(2,1)} %bitcast.21, bf16[2048,512]{1,0:T(8,128)(2,1)} %all-gather.7.cloned.1.call-done), kind=kOutput, calls=%fused_computation.8 | convolution fusion | flops 8592031744 | bytes 23068672 | tf_op jit(solution)/shard_map/dot_general | solution.py:30
  150.0 6.9 %reshape.36 = bf16[16,256,4,128]{3,2,1,0:T(4,128)(2,1)} reshape(bf16[4096,512]{1,0:T(8,128)(2,1)} %convolution_convert_fusion) | data formatting | bytes 8388608 | tf_op jit(solution)/shard_map/reshape | solution.py:72
  156.9 0.0 all-gather.5.cloned.1.call-done
  156.9 5.3 %fusion.19 = bf16[1024,512]{1,0:T(8,128)(2,1)S(1)} fusion(bf16[2048,512]{1,0:T(8,128)(2,1)} %all-gather.5.cloned.1.call-done, bf16[1024,2048]{1,0:T(8,128)(2,1)} %param.7, f32[1024]{0:T(1024)S(1)} %add_rsqrt_fusion), kind=kOutput, calls=%fused_computation.24 | convolution fusion | flops 2154299392 | bytes 7344128 | tf_op jit(solution)/shard_map/dot_general | solution.py:30
  162.2 0.5 reshape.35
  162.7 3.8 %fusion.7 = f32[16,4,64,256]{3,2,1,0:T(8,128)S(1)} fusion(bf16[16,256,4,128]{3,2,1,0:T(4,128)(2,1)} %reshape.36, bf16[16,64,4,128]{3,2,1,0:T(4,128)(2,1)S(1)} %reshape.35), kind=kOutput, calls=%fused_computation.13 | convolution fusion | flops 268435456 | bytes 9437184 | tf_op jit(solution)/shard_map/cmhd,cnhd->chmn/dot_general | solution.py:17
  166.5 0.0 copy-start.2
  166.5 1.9 copy-done.2
  168.4 1.6 fusion.35
  170.0 12.0 %fusion.22 = bf16[16,64,4,128]{3,1,2,0:T(8,128)(2,1)S(1)} fusion(bf16[16,256,4,128]{3,2,1,0:T(4,128)(2,1)} %reshape.34, f32[16,4,64]{2,1,0:T(4,128)S(1)} %fusion.35, f32[16,4,64,256]{3,2,1,0:T(8,128)} %copy-done.2), kind=kOutput, calls=%fused_computation.26 | convolution fusion | flops 274206976 | bytes 9453568 | tf_op jit(solution)/shard_map/chmn,cnhd->cmhd/dot_general | solution.py:23
  182.0 0.9 copy.18
  182.9 1.2 copy.33
  184.1 0.0 all-gather.9.cloned.1.call-update
  184.1 0.1 all-gather.11.cloned.1.call-done
  184.2 44.6 %all_to_all.19 = bf16[512,4,512]{0,2,1:T(8,128)(2,1)S(1)} all-to-all(bf16[512,4,512]{0,2,1:T(8,128)(2,1)} %bitcast.25), channel_id=1, replica_groups=mesh['seq'=4,'head'=4,'batch'=2] {'head'}, dimensions={1} | all-to-all | bytes 4194304 | tf_op jit(solution)/shard_map/all_to_all | solution.py:81
  228.8 2.4 copy.20
  231.1 6.4 %all-gather.9.cloned.1.call-done = bf16[1024,2048]{1,0:T(8,128)(2,1)} async-done(((bf16[1024,512]{1,0:T(8,128)(2,1)}), bf16[1024,2048]{1,0:T(8,128)(2,1)}) %all-gather.9.cloned.1.call-update) | async-done | bytes 4194320 | tf_op jit(solution)/shard_map/all_gather | solution.py:79
  237.5 6.2 %convolution_convert_fusion.2 = bf16[1024,512]{1,0:T(8,128)(2,1)} fusion(bf16[1024,2048]{1,0:T(8,128)(2,1)} %all-gather.9.cloned.1.call-done, bf16[2048,512]{1,0:T(8,128)(2,1)} %bitcast.26), kind=kOutput, calls=%fused_computation.25 | convolution fusion | flops 2148007936 | bytes 7340032 | tf_op jit(solution)/shard_map/dot_general | solution.py:82
  (11 shorter events, 0.3 us)
Async XLA Ops:
  6.5 129.1 %all-gather.7.cloned.1.call-start = ((), (), s32[]{:S(2)}) async-start(), calls=%async_computation.2 | async-start | bytes 2621440 | tf_op jit(solution)/shard_map/all_gather | solution.py:49
  7.3 149.7 %all-gather.5.cloned.1.call-start = ((), (), s32[]{:S(2)}) async-start(), calls=%async_computation.1 | async-start | bytes 2621440 | tf_op jit(solution)/shard_map/all_gather | solution.py:48
  7.3 50.8 %collective-permute-start.1 = (bf16[512,512]{1,0:T(8,128)(2,1)}, bf16[512,512]{1,0:T(8,128)(2,1)S(1)}, u32[]{:S(2)}, u32[]{:S(2)}) collective-permute-start(bf16[512,512]{1,0:T(8,128)(2,1)} %param.12), channel_id=1, source_target_pairs={{0,8},{8,16},{16,24},{24,0},{1,9},{9,17},{17,25},{25,1},{2,10},{10... | collective-permute-start | bytes 1572872 | tf_op jit(solution)/shard_map/ppermute | solution.py:59
  10.4 93.9 %collective-permute-start.3 = (bf16[512,512]{1,0:T(8,128)(2,1)}, bf16[512,512]{1,0:T(8,128)(2,1)S(1)}, u32[]{:S(2)}, u32[]{:S(2)}) collective-permute-start(bf16[512,512]{1,0:T(8,128)(2,1)} %param.12), channel_id=1, source_target_pairs={{0,24},{8,0},{16,8},{24,16},{1,25},{9,1},{17,9},{25,17},{2,26},{10... | collective-permute-start | bytes 1572872 | tf_op jit(solution)/shard_map/ppermute | solution.py:62
  12.5 171.7 %all-gather.11.cloned.1.call-start = ((), (), s32[]{:S(2)}) async-start(), calls=%async_computation.4 | async-start | bytes 2621440 | tf_op jit(solution)/shard_map/all_gather | solution.py:80
  13.2 13.3 %copy-start.5 = (s32[16]{0:T(128)S(1)}, s32[16]{0:T(128)}, u32[]{:S(2)}) copy-start(s32[16]{0:T(128)} %param.9) | copy-start | bytes 196
  26.5 17.0 %copy-start.4 = (bf16[512,512]{1,0:T(8,128)(2,1)S(1)}, bf16[512,512]{1,0:T(8,128)(2,1)}, u32[]{:S(2)}) copy-start(bf16[512,512]{1,0:T(8,128)(2,1)} %param.13) | copy-start | bytes 1572868
  35.2 5.7 %copy-start = (bf16[16,256,2048]{2,1,0:T(8,128)(2,1)}, bf16[16,256,2048]{2,1,0:T(8,128)(2,1)S(1)}, u32[]{:S(2)}) copy-start(bf16[16,256,2048]{2,1,0:T(8,128)(2,1)S(1)} %broadcast_select_fusion) | copy-start | bytes 50331652
  41.9 62.6 %collective-permute-start = (bf16[256,2048]{1,0:T(8,128)(2,1)}, bf16[256,2048]{1,0:T(8,128)(2,1)S(1)}, u32[]{:S(2)}, u32[]{:S(2)}) collective-permute-start(bf16[256,2048]{1,0:T(8,128)(2,1)} %slice_bitcast_fusion), channel_id=1, source_target_pairs={{0,8},{8,16},{16,24},{1,9},{9,17},{17,25},{2,10},{10,18},{18,26},{... | collective-permute-start | bytes 3145736 | tf_op jit(solution)/shard_map/ppermute | solution.py:13
  44.6 192.9 %all-gather.9.cloned.1.call-start = ((), (), s32[]{:S(2)}) async-start(), calls=%async_computation.3 | async-start | bytes 5242880 | tf_op jit(solution)/shard_map/all_gather | solution.py:79
  58.1 46.2 %copy-start.3 = (bf16[512,512]{1,0:T(8,128)(2,1)S(1)}, bf16[512,512]{1,0:T(8,128)(2,1)}, u32[]{:S(2)}) copy-start(bf16[512,512]{1,0:T(8,128)(2,1)} %param.12) | copy-start | bytes 1572868
  58.1 46.1 %collective-permute-start.2 = (bf16[512,512]{1,0:T(8,128)(2,1)S(1)}, bf16[512,512]{1,0:T(8,128)(2,1)S(1)}, u32[]{:S(2)}, u32[]{:S(2)}) collective-permute-start(bf16[512,512]{1,0:T(8,128)(2,1)S(1)} %collective-permute-done.1), channel_id=1, source_target_pairs={{0,8},{8,16},{16,24},{24,0},{1,9},{9,17},{17,25},{25,1},{2,10},{10... | collective-permute-start | bytes 1572872 | tf_op jit(solution)/shard_map/ppermute | solution.py:59
  112.5 5.7 %copy-start.1 = (bf16[16,256,2048]{2,1,0:T(8,128)(2,1)}, bf16[16,256,2048]{2,1,0:T(8,128)(2,1)S(1)}, u32[]{:S(2)}) copy-start(bf16[16,256,2048]{2,1,0:T(8,128)(2,1)S(1)} %pad_maximum_fusion) | copy-start | bytes 50331652
  166.5 2.0 copy-start.2
Sparse Core Ops, SparseCore 0:
  8.9 78.4 all-gather.6
  89.0 46.2 all-gather.4
  136.8 47.3 all-gather.10
  185.6 51.8 all-gather.8
